TPU v7x, 32 devices: a whole 2x2x4 slice. The times are simulated.
32 devices in a mesh: rep: 2 (over x), tp: 8 (over z, y), sub: 2 (over core).
Axes of the slice: x: 2, y: 2, z: 4, core: 2. Of those that a mesh axis runs over, the one named last changes fastest.
Arguments:
- attention: bfloat16 [1024, 8192], P('rep', ('tp', 'sub')), parts along dimension 0, may hold values from -6 to 6
- out_weight: bfloat16 [8192, 8192], P(('tp', 'sub')), may hold values from -0.09375 to 0.09375
- residual: bfloat16 [1024, 8192], P('rep', ('tp', 'sub')), parts along dimension 0, may hold values from -6 to 6
- norm_gain: bfloat16 [8192], P(('tp', 'sub')), may hold values from 0.25 to 1.75
Outputs:
- quantized: bfloat16 [1024, 8192], P('rep'), parts along dimension 0
- scales: bfloat16 [1024, 64], P('rep'), parts along dimension 0
- new_residual: bfloat16 [1024, 8192], P('rep', ('tp', 'sub')), parts along dimension 0
There are 2 independent parts, one for each index of `rep`. A program takes and returns all parts, laid end to end along the dimension named above; an argument that names none is the same for every part. Nothing has to cross between parts.
All inputs are finite; a program needn't handle non-finite values.
Results may differ from a plain program's by a relative error of at most 0.0048.
Values may be sent and summed in bfloat16 or wider, within the bound.
A program may use at most 128 MiB of HBM per device.

v0:
```python
import jax
import jax.numpy as jnp
from jax import lax
from jax.sharding import PartitionSpec as P

BLOCK = 128
epsilon = 0.1
floor_scale = 0.5


def per_device(attention, out_weight, residual, norm_gain):
    width_all = out_weight.shape[1]
    summed = lax.psum_scatter(
        lax.dot_general(
            out_weight, attention, (((0,), (1,)), ((), ())), preferred_element_type=jnp.float32
        ),
        ("tp", "sub"),
        scatter_dimension=0,
        tiled=True,
    )
    hidden = residual.astype(jnp.float32) + summed.T
    new_residual = hidden.astype(jnp.bfloat16)
    squares = lax.psum(jnp.sum(hidden * hidden, axis=1), ("tp", "sub"))
    mean_square = squares / width_all
    normed = hidden * lax.rsqrt(mean_square + epsilon)[:, None] * norm_gain.astype(jnp.float32)
    blocks = normed.reshape(hidden.shape[0], hidden.shape[1] // BLOCK, BLOCK)
    largest = jnp.max(jnp.abs(blocks), axis=2)
    scales = jnp.maximum(largest, floor_scale).astype(jnp.bfloat16)
    quantized = (
        (blocks / scales.astype(jnp.float32)[:, :, None]).reshape(hidden.shape).astype(jnp.bfloat16)
    )
    full_quant, full_scales = (
        lax.all_gather(quantized, ("tp", "sub"), axis=1, tiled=True),
        lax.all_gather(scales, ("tp", "sub"), axis=1, tiled=True),
    )
    return (full_quant, full_scales, new_residual)


def solution(mesh):
    in_specs = (
        P("rep", ("tp", "sub")),
        P(("tp", "sub"), None),
        P("rep", ("tp", "sub")),
        P(("tp", "sub")),
    )
    out_specs = (P("rep", None), P("rep", None), P("rep", ("tp", "sub")))
    return jax.shard_map(
        per_device, mesh=mesh, in_specs=in_specs, out_specs=out_specs, check_vma=False
    )
```

profile of v0, /device:TPU:0, one launch (start us, length us, event | category | flops | bytes accessed | tf_op | source)
XLA Modules:
  0.0 327.3 jit_solution(3654953643072817745)
XLA Ops:
  7.2 0.0 copy-start
  7.2 0.0 reduce-scatter.2.cloned.1.call-start
  7.2 1.0 copy-done
  8.2 11.7 %fusion.5 = f32[8192,512]{1,0:T(8,128)} fusion(bf16[512,8192]{1,0:T(8,128)(2,1)} %param.5, bf16[512,512]{1,0:T(8,128)(2,1)S(1)} %copy-done), kind=kOutput, calls=%fused_computation.12 | convolution fusion | flops 4294967296 | bytes 25690112 | tf_op jit(solution)/shard_map/dot_general | solution.py:14
  19.9 0.0 copy-start.1
  19.9 0.0 copy-start.2
  19.9 0.0 reduce-scatter.2.cloned.1.call-update
  19.9 0.0 all-gather.3.cloned.1.call-start
  20.0 1.0 copy-done.1
  20.9 0.2 copy.10
  21.2 0.0 copy-done.2
  21.2 179.0 %reduce-scatter.2.cloned.1.call-done = f32[512,512]{1,0:T(8,128)} async-done(((f32[8192,512]{1,0:T(8,128)}), f32[512,512]{1,0:T(8,128)}) %reduce-scatter.2.cloned.1.call-update) | async-done | bytes 1048592 | tf_op jit(solution)/shard_map/reduce_scatter | solution.py:13
  200.1 1.4 multiply_reduce_fusion
  201.5 31.5 %psum.7 = f32[512]{0:T(512)S(1)} all-reduce(f32[512]{0:T(512)S(1)} %multiply_reduce_fusion), channel_id=1, replica_groups=mesh['rep'=2,'tp'=8,'sub'=2] {'tp','sub'}, use_global_device_ids=true, to_apply=%region_2.0 | all-reduce | flops 512 | bytes 4096 | tf_op jit(solution)/shard_map/psum | solution.py:23
  233.1 1.4 bitcast_reduce_fusion
  234.5 2.2 fusion.2
  236.7 0.0 all-gather.3.cloned.1.call-update
  236.8 1.0 copy.12
  237.8 17.8 %all-gather = bf16[16,4,512]{2,1,0:T(4,128)(2,1)S(1)} all-gather(bf16[1,4,512]{2,1,0:T(4,128)(2,1)S(1)} %get-tuple-element.11), channel_id=1, replica_groups=mesh['rep'=2,'tp'=8,'sub'=2] {'tp','sub'}, dimensions={0}, use_global_device_ids=true | all-gather | bytes 69632 | tf_op jit(solution)/shard_map/all_gather | solution.py:34
  255.6 0.6 reshape.18
  256.2 52.3 %all-gather.3.cloned.1.call-done = bf16[512,8192]{0,1:T(8,128)(2,1)} async-done(((bf16[512,512]{0,1:T(8,128)(2,1)}), bf16[512,8192]{0,1:T(8,128)(2,1)}) %all-gather.3.cloned.1.call-update) | async-done | bytes 8388624 | tf_op jit(solution)/shard_map/all_gather | solution.py:33
  308.6 11.9 %copy.11 = bf16[512,8192]{1,0:T(8,128)(2,1)} copy(bf16[512,8192]{0,1:T(8,128)(2,1)} %all-gather.3.cloned.1.call-done) | data formatting | bytes 16777216
  (3 shorter events, 0.0 us)
Async XLA Ops:
  7.2 1.0 copy-start
  7.2 193.0 %reduce-scatter.2.cloned.1.call-start = ((), (), s32[]{:S(2)}) async-start(), calls=%async_computation.1 | async-start | bytes 17825792 | tf_op jit(solution)/shard_map/reduce_scatter | solution.py:13
  19.9 1.0 copy-start.1
  19.9 1.3 copy-start.2
  19.9 288.6 %all-gather.3.cloned.1.call-start = ((), (), s32[]{:S(2)}) async-start(), calls=%async_computation.2 | async-start | bytes 8912896 | tf_op jit(solution)/shard_map/all_gather | solution.py:33
Sparse Core Ops, SparseCore 0:
  20.0 180.0 reduce-scatter.1
  236.9 71.6 all-gather.2
where the time goes:
time: 328 us; the launch traced here: 327 us
  waiting for transfers between devices  231 us (70%)
  blocking collectives  49.3 us (15%)
  local copies, waits for them, and re-layouts  15.7 us (5%)
  between operations  14.1 us (4%)
  matrix products  11.7 us (4%)
  other arithmetic  5.1 us (2%)
    reduce_scatter x1, waiting for transfers between devices, per_device(): lax.psum_scatter(lax.dot_general(out_weight, attention, (((0,), (1,)), ((...  179 us
    all_gather x1, waiting for transfers between devices, per_device(): lax.all_gather(quantized, ('tp', 'sub'), axis=1, tiled=True)  52.3 us
    psum x1, blocking collectives, per_device(): squares = lax.psum(jnp.sum(hidden * hidden, axis=1), ('tp', 'sub'))  31.5 us
    all_gather x1, blocking collectives, per_device(): lax.all_gather(scales, ('tp', 'sub'), axis=1, tiled=True)  17.8 us
    unnamed x10, local copies, waits for them, and re-layouts  15.7 us
    dot_general x1, matrix products, per_device(): lax.dot_general(out_weight, attention, (((0,), (1,)), ((), ())), preferre...  11.7 us
  transfers between devices with their start and end apart: 2, of which 2 were waited for; matrix products, arithmetic and copies ran while one was open for 1% of the time, Pallas kernels for 0%

commit v1 on v0

--- a/solution.py
+++ b/solution.py
@@ -20,7 +20,9 @@
     )
     hidden = residual.astype(jnp.float32) + summed.T
     new_residual = hidden.astype(jnp.bfloat16)
-    squares = lax.psum(jnp.sum(hidden * hidden, axis=1), ("tp", "sub"))
+    part = jnp.sum(hidden * hidden, axis=1)
+    parts = lax.all_gather(part, ("tp", "sub"))
+    squares = jnp.sum(parts, axis=0)
     mean_square = squares / width_all
     normed = hidden * lax.rsqrt(mean_square + epsilon)[:, None] * norm_gain.astype(jnp.float32)
     blocks = normed.reshape(hidden.shape[0], hidden.shape[1] // BLOCK, BLOCK)

time: 328 us -> 316 us (0.963)
  blocking collectives: 49.3 us -> 37.6 us
    psum x1 -> x0, blocking collectives: 31.5 us -> none  [per_device(): squares = lax.psum(jnp.sum(hidden * hidden, axis=1), ('tp', 'sub'))]
    all_gather x0 -> x1, blocking collectives: none -> 19.5 us  [per_device(): parts = lax.all_gather(part, ('tp', 'sub'))]
where the time goes in v1:
time: 316 us; the launch traced here: 315 us
  waiting for transfers between devices  231 us (73%)
  blocking collectives  37.6 us (12%)
  local copies, waits for them, and re-layouts  15.7 us (5%)
  between operations  14.1 us (4%)
  matrix products  11.7 us (4%)
  other arithmetic  5.14 us (2%)
    reduce_scatter x1, waiting for transfers between devices, per_device(): lax.psum_scatter(lax.dot_general(out_weight, attention, (((0,), (1,)), ((...  179 us
    all_gather x1, waiting for transfers between devices, per_device(): lax.all_gather(quantized, ('tp', 'sub'), axis=1, tiled=True)  52.1 us
    all_gather x1, blocking collectives, per_device(): parts = lax.all_gather(part, ('tp', 'sub'))  19.5 us
    all_gather x1, blocking collectives, per_device(): lax.all_gather(scales, ('tp', 'sub'), axis=1, tiled=True)  18.1 us
    unnamed x10, local copies, waits for them, and re-layouts  15.7 us
    dot_general x1, matrix products, per_device(): lax.dot_general(out_weight, attention, (((0,), (1,)), ((), ())), preferre...  11.7 us
  transfers between devices with their start and end apart: 2, of which 2 were waited for; matrix products, arithmetic and copies ran while one was open for 1% of the time, Pallas kernels for 0%

profile of v1, /device:TPU:0, one launch (start us, length us, event | category | flops | bytes accessed | tf_op | source)
XLA Modules:
  0.0 315.4 jit_solution(3037648148425405760)
XLA Ops:
  7.2 0.0 copy-start
  7.2 0.0 reduce-scatter.2.cloned.1.call-start
  7.2 1.0 copy-done
  8.2 11.7 %fusion.5 = f32[8192,512]{1,0:T(8,128)} fusion(bf16[512,8192]{1,0:T(8,128)(2,1)} %param.5, bf16[512,512]{1,0:T(8,128)(2,1)S(1)} %copy-done), kind=kOutput, calls=%fused_computation.12 | convolution fusion | flops 4294967296 | bytes 25690112 | tf_op jit(solution)/shard_map/dot_general | solution.py:14
  19.9 0.0 copy-start.1
  19.9 0.0 copy-start.2
  19.9 0.0 reduce-scatter.2.cloned.1.call-update
  19.9 0.0 all-gather.5.cloned.1.call-start
  20.0 1.0 copy-done.1
  20.9 0.2 copy.10
  21.2 0.0 copy-done.2
  21.2 179.0 %reduce-scatter.2.cloned.1.call-done = f32[512,512]{1,0:T(8,128)} async-done(((f32[8192,512]{1,0:T(8,128)}), f32[512,512]{1,0:T(8,128)}) %reduce-scatter.2.cloned.1.call-update) | async-done | bytes 1048592 | tf_op jit(solution)/shard_map/reduce_scatter | solution.py:13
  200.1 1.4 multiply_reduce_fusion
  201.5 19.5 %all-gather.1 = f32[16,1,512]{2,1,0:T(1,128)S(1)} all-gather(f32[1,1,512]{2,1,0:T(1,128)S(1)} %bitcast.25), channel_id=2, replica_groups=mesh['rep'=2,'tp'=8,'sub'=2] {'tp','sub'}, dimensions={0}, use_global_device_ids=true | all-gather | bytes 34816 | tf_op jit(solution)/shard_map/all_gather | solution.py:24
  221.1 1.4 bitcast_reduce_fusion
  222.6 2.2 fusion.2
  224.8 0.0 all-gather.5.cloned.1.call-update
  224.8 1.0 copy.12
  225.8 18.1 %all-gather.2 = bf16[16,4,512]{2,1,0:T(4,128)(2,1)S(1)} all-gather(bf16[1,4,512]{2,1,0:T(4,128)(2,1)S(1)} %get-tuple-element.11), channel_id=1, replica_groups=mesh['rep'=2,'tp'=8,'sub'=2] {'tp','sub'}, dimensions={0}, use_global_device_ids=true | all-gather | bytes 69632 | tf_op jit(solution)/shard_map/all_gather | solution.py:36
  244.0 0.6 reshape.25
  244.6 52.1 %all-gather.5.cloned.1.call-done = bf16[512,8192]{0,1:T(8,128)(2,1)} async-done(((bf16[512,512]{0,1:T(8,128)(2,1)}), bf16[512,8192]{0,1:T(8,128)(2,1)}) %all-gather.5.cloned.1.call-update) | async-done | bytes 8388624 | tf_op jit(solution)/shard_map/all_gather | solution.py:35
  296.7 11.9 %copy.11 = bf16[512,8192]{1,0:T(8,128)(2,1)} copy(bf16[512,8192]{0,1:T(8,128)(2,1)} %all-gather.5.cloned.1.call-done) | data formatting | bytes 16777216
  (4 shorter events, 0.1 us)
Async XLA Ops:
  7.2 1.0 copy-start
  7.2 193.0 %reduce-scatter.2.cloned.1.call-start = ((), (), s32[]{:S(2)}) async-start(), calls=%async_computation.1 | async-start | bytes 17825792 | tf_op jit(solution)/shard_map/reduce_scatter | solution.py:13
  19.9 1.0 copy-start.1
  19.9 1.3 copy-start.2
  19.9 276.8 %all-gather.5.cloned.1.call-start = ((), (), s32[]{:S(2)}) async-start(), calls=%async_computation.2 | async-start | bytes 8912896 | tf_op jit(solution)/shard_map/all_gather | solution.py:35
Sparse Core Ops, SparseCore 0:
  20.0 180.0 reduce-scatter.1
  224.9 71.6 all-gather.4
